TPU v7x, 32 devices: a whole 2x2x4 slice. The times are simulated.
32 devices in a mesh: theta: 4 (over y, core), phi: 8 (over z, x).
Axes of the slice: x: 2, y: 2, z: 4, core: 2. Of those that a mesh axis runs over, the one named last changes fastest.
Arguments:
- fields: float32 [8, 2, 1024, 4096], P(None, None, 'theta', 'phi'), may hold values from -6 to 6
- legendre: float32 [1024, 512, 1025], P('theta', 'phi'), may hold values from -0.0029296875 to 0.0029296875
- pair_table: int32 [512], replicated, may hold values from 0 to 511, each once
Outputs:
- coefficients: float32 [512, 2, 8, 1025], P(('phi', 'theta'))
Inputs may be any that keep to these rules, and one draw needn't show every extreme that they name: A permutation: slot s holds the orders 1024 + pair_table[s] and 2047 - pair_table[s].
All inputs are finite; a program needn't handle non-finite values.
Results may differ from a plain program's by a relative error of at most 0.0003.
Values sent between devices are 32-bit elements; how exact they have to be, the bound alone decides.
A program may use at most 192 MiB of HBM per device.

v0:
```python
import math

import jax
import jax.numpy as jnp
from jax import lax
from jax.sharding import PartitionSpec as P

LONS = 4096
DEGREES = 2048
ORDERS = 1024
LOW_ORDER = 1024
PAIR_LEN = 1025


full_precision = lax.Precision.HIGHEST


def order_pairs(pairs):
    return jnp.stack([LOW_ORDER + pairs, DEGREES - 1 - pairs], axis=0)


def transform(flat, orders, longitudes):
    product = longitudes[:, None, None] * orders[None, :, :] % LONS
    angles = product.astype(jnp.float32) * (2.0 * math.pi / LONS)
    cosines = jnp.cos(angles)
    sines = -jnp.sin(angles)
    real_part = jnp.einsum("rk,kan->nar", flat, cosines, precision=full_precision)
    imag_part = jnp.einsum("rk,kan->nar", flat, sines, precision=full_precision)
    return jnp.stack([real_part, imag_part], axis=1)


def order_masks(pairs):
    columns = jnp.arange(PAIR_LEN, dtype=jnp.int32)[None, :]
    shifts = pairs[:, None]
    first = columns < ORDERS - shifts
    parity = jnp.where(first, columns % 2, (columns + shifts) % 2) == 0
    even_rows = jnp.stack([first & parity, ~first & parity], axis=1)
    odd_rows = jnp.stack([first & ~parity, ~first & ~parity], axis=1)
    return jnp.stack([even_rows, odd_rows], axis=1).astype(jnp.float32)


def on_device(fields, legendre, pair_table):
    field_count = fields.shape[0]
    lat_count = fields.shape[2]
    lon_count = fields.shape[3]
    slot_count = legendre.shape[1]
    row_count = field_count * 2 * lat_count
    phi_index = lax.axis_index("phi")
    own_pairs = lax.dynamic_slice_in_dim(pair_table, phi_index * slot_count, slot_count)
    flat = fields.reshape(row_count, lon_count)
    cycles = lax.all_to_all(flat, "phi", split_axis=0, concat_axis=1, tiled=True)
    longitudes = jnp.arange(LONS, dtype=jnp.int32)
    spectra = transform(cycles, order_pairs(pair_table), longitudes)
    grouped = lax.all_to_all(spectra, "phi", split_axis=0, concat_axis=3, tiled=True)
    grouped = grouped.reshape(slot_count, 2, 2, field_count, 2, lat_count)
    north = grouped[:, :, :, :, 0]
    south = grouped[:, :, :, :, 1]
    variants = jnp.stack([north + south, north - south], axis=1).reshape(
        slot_count, 8 * field_count, lat_count
    )
    masks = order_masks(own_pairs)
    theta_count = lax.axis_size("theta")
    product = lax.dot_general(
        variants,
        legendre,
        (((2,), (0,)), ((0,), (1,))),
        precision=full_precision,
        preferred_element_type=jnp.float32,
    )
    product = product.reshape(
        slot_count // theta_count * lax.axis_size("theta"), 2, 2, 2, field_count, PAIR_LEN
    )
    return lax.psum_scatter(
        jnp.sum(product * masks[:, :, None, :, None, :], axis=(1, 3)),
        "theta",
        scatter_dimension=0,
        tiled=True,
    )


def solution(mesh):
    placed = (P(None, None, "theta", "phi"), P("theta", "phi", None), P())
    return jax.shard_map(
        on_device,
        mesh=mesh,
        in_specs=placed,
        out_specs=P(("phi", "theta"), None, None, None),
        check_vma=False,
    )
```

profile of v0, /device:TPU:0, one launch (start us, length us, event | category | flops | bytes accessed | tf_op | source)
XLA Modules:
  0.0 561.4 jit_solution(4292950005836192562)
XLA Ops:
  6.5 7.4 %all-to-all-start = ((f32[8,512,512]{2,1,0:T(8,128)}), f32[8,512,512]{2,1,0:T(8,128)}, u32[]{:S(2)}, u32[]{:S(2)}) async-start(f32[8,512,512]{2,1,0:T(8,128)} %bitcast.42), calls=%async_computation | async-start | bytes 16777216 | tf_op jit(solution)/shard_map/all_to_all | solution.py:51
  14.0 64.3 %fusion.45 = f32[4096,2,512]{0,2,1:T(8,128)} fusion(s32[2,512]{1,0:T(2,128)S(1)} %pad_add_fusion), kind=kLoop, calls=%fused_computation.13.clone.clone.clone.1 | loop fusion | flops 58720256 | bytes 16781312 | tf_op jit(solution)/shard_map/rk,kan->nar/dot_general | solution.py:27
  78.3 65.3 %fusion.47 = f32[4096,2,512]{0,2,1:T(8,128)} fusion(s32[2,512]{1,0:T(2,128)S(1)} %pad_add_fusion), kind=kLoop, calls=%fused_computation.10.clone.clone.clone.1 | loop fusion | flops 62914560 | bytes 16781312 | tf_op jit(solution)/shard_map/rk,kan->nar/dot_general | solution.py:28
  143.5 53.6 %all-to-all-done = f32[8,512,512]{2,1,0:T(8,128)} async-done(((f32[8,512,512]{2,1,0:T(8,128)}), f32[8,512,512]{2,1,0:T(8,128)}, u32[]{:S(2)}, u32[]{:S(2)}) %all-to-all-start) | async-done | bytes 8388640 | tf_op jit(solution)/shard_map/all_to_all | solution.py:51
  197.1 11.5 %copy.15 = f32[512,8,512]{2,1,0:T(8,128)} copy(f32[512,8,512]{2,0,1:T(8,128)} %bitcast.3) | data formatting | bytes 16777216 | tf_op jit(solution)/shard_map/all_to_all | solution.py:51
  208.6 9.4 %reshape.385 = f32[512,4096,1]{1,0,2:T(8,128)} reshape(f32[512,8,512]{2,1,0:T(8,128)} %copy.15) | data formatting | bytes 16777216 | tf_op jit(solution)/shard_map/all_to_all | solution.py:51
  217.9 30.6 %fusion.18 = f32[512,1,2,512]{3,0,2,1:T(8,128)S(1)} fusion(f32[512,4096,1]{1,0,2:T(8,128)} %reshape.385, f32[4096,2,512]{0,2,1:T(8,128)} %fusion.47), kind=kOutput, calls=%fused_computation.24 | convolution fusion | flops 25769803776 | bytes 27262976 | tf_op jit(solution)/shard_map/rk,kan->nar/dot_general | solution.py:28
  248.5 29.5 %fusion.15 = f32[512,1,2,512]{3,0,2,1:T(8,128)S(1)} fusion(f32[512,4096,1]{1,0,2:T(8,128)S(1)} %copy-done, f32[4096,2,512]{0,2,1:T(8,128)} %fusion.45), kind=kOutput, calls=%fused_computation.23 | convolution fusion | flops 25769803776 | bytes 27262976 | tf_op jit(solution)/shard_map/rk,kan->nar/dot_general | solution.py:27
  278.0 0.4 pad_maximum_fusion
  278.4 5.2 copy.16
  283.7 4.6 all-to-all-start.1
  288.3 0.1 broadcast_subtract_fusion.1
  288.4 3.0 fusion.24
  291.4 1.4 add_bitcast_fusion.1
  292.8 0.6 add_convert_fusion
  293.4 87.3 %all-to-all-done.1 = f32[512,2,2,512]{3,2,1,0:T(2,128)} async-done(((f32[512,2,2,512]{3,2,1,0:T(2,128)}), f32[512,2,2,512]{3,2,1,0:T(2,128)}, u32[]{:S(2)}, u32[]{:S(2)}) %all-to-all-start.1) | async-done | bytes 4194336 | tf_op jit(solution)/shard_map/all_to_all | solution.py:54
  380.8 6.6 %copy.24 = f32[8,64,2,2,512]{4,0,3,2,1:T(8,128)} copy(f32[8,64,2,2,512]{4,3,2,1,0:T(2,128)} %bitcast.8) | data formatting | bytes 8388608 | tf_op jit(solution)/shard_map/all_to_all | solution.py:54
  387.4 5.9 %reshape.382 = f32[64,2,2,8,2,256]{5,4,3,2,1,0:T(2,128)} reshape(f32[64,2,2,8,512]{4,3,2,1,0:T(8,128)} %bitcast.41) | data formatting | bytes 8388608 | tf_op jit(solution)/shard_map/reshape | solution.py:55
  393.2 7.4 %add_bitcast_fusion = (f32[64,1,2,2,8,256]{5,1,4,3,2,0:T(1,128)S(1)}, f32[64,1,2,2,8,256]{5,1,4,3,2,0:T(1,128)S(1)}) fusion(f32[64,2,2,8,2,256]{5,4,3,2,1,0:T(2,128)} %reshape.382), kind=kLoop, calls=%fused_computation.22 | loop fusion | flops 1048576 | bytes 8388608 | tf_op jit(solution)/shard_map/add | solution.py:58
  400.7 4.3 pad_maximum_fusion.1
  405.0 0.7 copy.18
  405.6 90.8 %fusion = f32[64,64,1025]{2,1,0:T(8,128)} fusion(f32[64,64,256]{2,1,0:T(8,128)S(1)} %bitcast.40, f32[256,64,1025]{0,1,2:T(8,128)} %param.4), kind=kOutput, calls=%fused_computation | convolution fusion | flops 12897484800 | bytes 88162304 | tf_op jit(solution)/shard_map/dot_general | solution.py:63
  496.4 10.4 %multiply_reduce_fusion = f32[64,2,8,1025]{3,2,1,0:T(8,128)} fusion(f32[64,2,2,2,8,1025]{5,4,3,2,1,0:T(8,128)} %bitcast.39, f32[64,2,2,1025]{3,2,1,0:T(2,128)S(1)} %add_convert_fusion), kind=kLoop, calls=%fused_computation.5 | loop fusion | flops 7347200 | bytes 22041600 | tf_op jit(solution)/shard_map/reduce_sum | solution.py:74
  506.9 47.2 %reduce-scatter.2.cloned.1.call-done = f32[16,2,8,1025]{3,2,1,0:T(8,128)} async-done(((f32[64,2,8,1025]{3,2,1,0:T(8,128)}), f32[16,2,8,1025]{3,2,1,0:T(8,128)}) %reduce-scatter.2.cloned.1.call-update) | async-done | bytes 1049616 | tf_op jit(solution)/shard_map/reduce_scatter | solution.py:73
  (9 shorter events, 0.1 us)
Async XLA Ops:
  6.5 7.4 %copy-start.1 = (s32[512]{0:T(512)S(1)}, s32[512]{0:T(512)}, u32[]{:S(2)}) copy-start(s32[512]{0:T(512)} %param.5) | copy-start | bytes 6148
  6.5 190.6 %all-to-all-start = ((f32[8,512,512]{2,1,0:T(8,128)}), f32[8,512,512]{2,1,0:T(8,128)}, u32[]{:S(2)}, u32[]{:S(2)}) async-start(f32[8,512,512]{2,1,0:T(8,128)} %bitcast.42), calls=%async_computation | async-start | bytes 16777216 | tf_op jit(solution)/shard_map/all_to_all | solution.py:51
  217.9 30.6 %copy-start = (f32[512,4096,1]{1,0,2:T(8,128)S(1)}, f32[512,4096,1]{1,0,2:T(8,128)}, u32[]{:S(2)}) copy-start(f32[512,4096,1]{1,0,2:T(8,128)} %reshape.385) | copy-start | bytes 25165828
  283.7 97.1 %all-to-all-start.1 = ((f32[512,2,2,512]{3,2,1,0:T(2,128)}), f32[512,2,2,512]{3,2,1,0:T(2,128)}, u32[]{:S(2)}, u32[]{:S(2)}) async-start(f32[512,2,2,512]{3,2,1,0:T(2,128)} %copy.16), calls=%async_computation.1 | async-start | bytes 8388608 | tf_op jit(solution)/shard_map/all_to_all | solution.py:54
  288.2 265.9 %reduce-scatter.2.cloned.1.call-start = ((), (), s32[]{:S(2)}) async-start(), calls=%async_computation.3 | async-start | bytes 5898240 | tf_op jit(solution)/shard_map/reduce_scatter | solution.py:73
Sparse Core Ops, SparseCore 0:
  507.0 47.0 reduce-scatter.1
where the time goes:
time: 569 us; the launch traced here: 561 us
  waiting for transfers between devices  188 us (33%)
  other arithmetic  157 us (28%)
  matrix products  151 us (27%)
  local copies, waits for them, and re-layouts  39.2 us (7%)
  between operations  14 us (2%)
  starting transfers between devices  12 us (2%)
    dot_general x1, matrix products, on_device(): lax.dot_general(variants, legendre, (((2,), (0,)), ((0,), (1,))), precisi...  90.8 us
    all_to_all x1, waiting for transfers between devices, on_device(): lax.all_to_all(spectra, 'phi', split_axis=0, concat_axis=3, tiled=True)  87.3 us
    dot_general x1, other arithmetic, transform(): imag_part = jnp.einsum('rk,kan->nar', flat, sines, precision=full_precision)  65.3 us
    dot_general x1, other arithmetic, transform(): jnp.einsum('rk,kan->nar', flat, cosines, precision=full_precision)  64.3 us
    all_to_all x1, waiting for transfers between devices, on_device(): lax.all_to_all(flat, 'phi', split_axis=0, concat_axis=1, tiled=True)  53.6 us
    reduce_scatter x1, waiting for transfers between devices, on_device(): lax.psum_scatter(jnp.sum(product * masks[:, :, None, :, None, :], axis=(1...  47.2 us
    dot_general x1, matrix products, transform(): imag_part = jnp.einsum('rk,kan->nar', flat, sines, precision=full_precision)  30.6 us
    dot_general x1, matrix products, transform(): jnp.einsum('rk,kan->nar', flat, cosines, precision=full_precision)  29.5 us
  transfers between devices with their start and end apart: 3, of which 3 were waited for; matrix products, arithmetic and copies ran while one was open for 24% of the time, Pallas kernels for 0%

commit v1 on v0

v1 whole, which is shorter than its diff:
```python
import math

import jax
import jax.numpy as jnp
import numpy as np
from jax import lax
from jax.sharding import PartitionSpec as P

high = lax.Precision.HIGH


def add(x, y, sign=1.0):
    re = x[0] + y[0] if sign > 0 else x[0] - y[0]
    if x[1] is None and y[1] is None:
        return re, None
    if y[1] is None:
        return re, x[1]
    im = y[1] if sign > 0 else -y[1]
    return re, im if x[1] is None else x[1] + im


def turn(x, step, count):
    if step == 0:
        return x
    if 4 * step == count:
        return (x[1], -x[0]) if x[1] is not None else (jnp.zeros_like(x[0]), -x[0])
    c = float(math.cos(2 * math.pi * step / count))
    s = float(math.sin(2 * math.pi * step / count))
    if x[1] is None:
        return x[0] * c, x[0] * -s
    return x[0] * c + x[1] * s, x[1] * c - x[0] * s


def butterfly(parts):
    count = len(parts)
    if count == 1:
        return [parts[0]]
    low = butterfly(parts[0::2])
    odd = butterfly(parts[1::2])
    odd = [turn(x, i, count) for i, x in enumerate(odd)]
    return [add(x, y) for x, y in zip(low, odd)] + [add(x, y, -1.0) for x, y in zip(low, odd)]


def half_residues(parts):
    count = len(parts)
    found = butterfly([(x, None) for x in parts])
    for i in range(count // 2 + 1, count):
        re, im = found[count - i]
        found[i] = (re, -im if im is not None else None)
    return found


def on_device(fields, legendre, pair_table):
    field_count, _, lat_count, lon_count = fields.shape
    slot_count, pair_len = legendre.shape[1], legendre.shape[2]
    phi, theta = lax.axis_size("phi"), lax.axis_size("theta")
    pairs = pair_table.shape[0]
    orders = 2 * pairs
    low_order = pair_len - 1
    lons = lon_count * phi
    row_count = field_count * 2 * lat_count
    chunk = row_count // phi
    per = orders // phi

    flat = fields.reshape(phi, chunk, lon_count)
    cycles = lax.all_to_all(flat, "phi", split_axis=0, concat_axis=0, tiled=True)

    residues = half_residues([cycles[p] for p in range(phi)])
    k = np.arange(lon_count)
    rows = []
    for m0, (re, im) in enumerate(residues):
        c = jnp.asarray(np.cos(2 * np.pi * m0 * k / lons), jnp.float32)
        s = jnp.asarray(np.sin(2 * np.pi * m0 * k / lons), jnp.float32)
        if m0 == 0:
            zr, zi = re, jnp.zeros_like(re) if im is None else im
        elif im is None:
            zr, zi = re * c, -re * s
        else:
            zr, zi = re * c + im * s, im * c - re * s
        rows.append(jnp.concatenate([zr, zi], axis=1))
    stacked = jnp.concatenate(rows, axis=0)
    m1 = low_order // phi + np.arange(per)
    angles = 2 * np.pi * (np.outer(m1, k) % lon_count) / lon_count
    c, s = np.cos(angles), np.sin(angles)
    weights = jnp.asarray(np.block([[c, s], [-s, c]]), jnp.float32)
    spectra = lax.dot_general(
        weights, stacked, (((1,), (1,)), ((), ())), precision=high, preferred_element_type=jnp.float32
    ).reshape(2, orders, chunk)

    wanted = jnp.stack([pair_table, orders - 1 - pair_table], axis=1).reshape(orders)
    pick = (wanted[:, None] == jnp.arange(orders, dtype=jnp.int32)[None, :]).astype(jnp.float32)
    chosen = jnp.stack(
        [
            lax.dot_general(pick, spectra[r], (((1,), (0,)), ((), ())), precision=high,
                            preferred_element_type=jnp.float32)
            for r in range(2)
        ],
        axis=1,
    )
    grouped = lax.all_to_all(
        chosen.reshape(phi, slot_count, 2, 2, chunk), "phi", split_axis=0, concat_axis=0, tiled=True
    )
    grouped = jnp.moveaxis(grouped, 0, 3).reshape(slot_count, 2, 2, field_count, 2, lat_count)
    north, south = grouped[:, :, :, :, 0], grouped[:, :, :, :, 1]
    variants = jnp.stack([north + south, north - south], axis=1).reshape(
        slot_count, 8 * field_count, lat_count
    )
    product = lax.dot_general(
        variants, legendre, (((2,), (0,)), ((0,), (1,))), precision=high,
        preferred_element_type=jnp.float32,
    ).reshape(slot_count, 2, 2, 2, field_count, pair_len)

    own = lax.dynamic_slice_in_dim(pair_table, lax.axis_index("phi") * slot_count, slot_count)
    columns = jnp.arange(pair_len, dtype=jnp.int32)[None, :]
    shifts = own[:, None]
    first = columns < orders - shifts
    even = jnp.where(first, columns % 2, (columns + shifts) % 2) == 0
    first = first[:, None, None, :]
    even = even[:, None, None, :]
    result = jnp.where(
        first,
        jnp.where(even, product[:, 0, 0], product[:, 1, 0]),
        jnp.where(even, product[:, 0, 1], product[:, 1, 1]),
    )
    return lax.psum_scatter(result, "theta", scatter_dimension=0, tiled=True)


def solution(mesh):
    placed = (P(None, None, "theta", "phi"), P("theta", "phi", None), P())
    return jax.shard_map(
        on_device,
        mesh=mesh,
        in_specs=placed,
        out_specs=P(("phi", "theta"), None, None, None),
        check_vma=False,
    )
```

time: 569 us -> 530 us (0.931)
  waiting for transfers between devices: 188 us -> 322 us
  other arithmetic: 157 us -> 30.7 us
  matrix products: 151 us -> 118 us
  local copies, waits for them, and re-layouts: 39.2 us -> 24.7 us
    all_to_all x2, waiting for transfers between devices: 141 us -> 275 us  [the longest x1 183 us: on_device(): lax.all_to_all(flat, 'phi', split_axis=0, concat_axis=0, tiled=True)]
    dot_general x2 -> x0, other arithmetic: 130 us -> none  [the longest x1 65.3 us: transform(): imag_part = jnp.einsum('rk,kan->nar', flat, sines, precision=full_precision)]
    dot_general x2 -> x3, matrix products: 60 us -> 25.5 us  [the longest x1 19 us: on_device(): lax.dot_general(weights, stacked, (((1,), (1,)), ((), ())), precision=hig...]
    all_to_all x3 -> x0, local copies, waits for them, and re-layouts: 27.4 us -> none  [the longest x2 20.8 us: on_device(): lax.all_to_all(flat, 'phi', split_axis=0, concat_axis=1, tiled=True)]
    add x1 -> x7, other arithmetic: 0.01 us -> 16.3 us  [the longest x6 16.1 us: on_device(): zr, zi = (re * c + im * s, im * c - re * s)]
    reduce_sum x1 -> x0, other arithmetic: 10.4 us -> none  [on_device(): jnp.sum(product * masks[:, :, None, :, None, :], axis=(1, 3))]
    slice x0 -> x2, local copies, waits for them, and re-layouts: none -> 9.52 us  [the longest x1 7.82 us: on_device(): north, south = (grouped[:, :, :, :, 0], grouped[:, :, :, :, 1])]
    select_n x1 -> x2, other arithmetic: 0.01 us -> 9.49 us  [the longest x1 9.48 us: on_device(): jnp.where(first, jnp.where(even, product[:, 0, 0], product[:, 1, 0]), jnp...]
  transfers between devices with their start and end apart: 3 -> 3, of which waited for: 3 -> 3; matrix products, arithmetic and copies ran while one was open for 24% -> 0% of each run, Pallas kernels for 0% -> 0%
where the time goes in v1:
time: 530 us; the launch traced here: 522 us
  waiting for transfers between devices  322 us (61%)
  matrix products  118 us (22%)
  other arithmetic  30.7 us (6%)
  local copies, waits for them, and re-layouts  24.7 us (5%)
  between operations  14.1 us (3%)
  starting transfers between devices  12 us (2%)
    all_to_all x1, waiting for transfers between devices, on_device(): lax.all_to_all(flat, 'phi', split_axis=0, concat_axis=0, tiled=True)  183 us
    dot_general x1, matrix products, on_device(): lax.dot_general(variants, legendre, (((2,), (0,)), ((0,), (1,))), precisi...  92.2 us
    all_to_all x1, waiting for transfers between devices, on_device(): lax.all_to_all(chosen.reshape(phi, slot_count, 2, 2, chunk), 'phi', split...  92.1 us
    reduce_scatter x1, waiting for transfers between devices, on_device(): return lax.psum_scatter(result, 'theta', scatter_dimension=0, tiled=True)  47.2 us
    dot_general x1, matrix products, on_device(): lax.dot_general(weights, stacked, (((1,), (1,)), ((), ())), precision=hig...  19 us
    add x6, other arithmetic, on_device(): zr, zi = (re * c + im * s, im * c - re * s)  16.1 us
  transfers between devices with their start and end apart: 3, of which 3 were waited for; matrix products, arithmetic and copies ran while one was open for 0% of the time, Pallas kernels for 0%

profile of v1, /device:TPU:0, one launch (start us, length us, event | category | flops | bytes accessed | tf_op | source)
XLA Modules:
  0.0 521.5 jit_solution(4764979156779760669)
XLA Ops:
  6.5 7.4 %all-to-all-start = ((f32[8,512,512]{2,1,0:T(8,128)}), f32[8,512,512]{2,1,0:T(8,128)}, u32[]{:S(2)}, u32[]{:S(2)}) async-start(f32[8,512,512]{2,1,0:T(8,128)} %bitcast.151), calls=%async_computation | async-start | bytes 16777216 | tf_op jit(solution)/shard_map/all_to_all | solution.py:66
  14.2 182.9 %all-to-all-done = f32[8,512,512]{2,1,0:T(8,128)} async-done(((f32[8,512,512]{2,1,0:T(8,128)}), f32[8,512,512]{2,1,0:T(8,128)}, u32[]{:S(2)}, u32[]{:S(2)}) %all-to-all-start) | async-done | bytes 8388640 | tf_op jit(solution)/shard_map/all_to_all | solution.py:66
  197.1 4.5 fusion.35
  201.6 5.8 %fusion.27 = (f32[512,512]{1,0:T(8,128)S(1)}, f32[1,512,512]{2,1,0:T(8,128)S(1)}, f32[1,512,512]{2,1,0:T(8,128)}, f32[512,512]{1,0:T(8,128)S(1)}, f32[1,512,512]{2,1,0:T(8,128)S(1)}, /*index=5*/f32[1,512,512]{2,1,0:T(8,128)S(1)}) fusion(f32[512]{0:T(512)S(1)} %copy-done.8, f32[512]{0:T(512)S(1)} %copy-done.9, f32[1,512,512]{2,1,0:T(8,128)S(1)} %get-tuple-element.11, ...), kind=kLoop, calls=%fused_computation.43 | loop fusion | flops 5767168 | bytes 16783360 | tf_op jit(solution)/shard_map/add | solution.py:79
  208.8 4.5 fusion.29
  213.9 0.7 copy-done
  214.6 0.5 fusion.25
  216.0 0.9 copy-done.2
  216.8 19.0 %fusion.56 = f32[256,4096]{1,0:T(8,128)S(1)} fusion(f32[256,1024]{1,0:T(8,128)S(1)} %copy-done.2, f32[4096,1024]{1,0:T(8,128)S(1)} %maximum_dynamic-update-slice_fusion), kind=kOutput, calls=%fused_computation.105 | convolution fusion | flops 6442450944 | bytes 22020096 | tf_op jit(solution)/shard_map/dot_general | solution.py:86
  235.9 1.7 fusion.55
  237.6 2.8 reshape.240
  240.4 1.5 reshape.241
  241.9 4.1 fusion.14
  246.0 2.4 fusion.19
  248.4 0.7 pad_maximum_fusion
  249.1 2.6 copy.28
  251.7 4.5 all-to-all-start.1
  256.7 92.1 %all-to-all-done.1 = f32[8,64,2,2,512]{4,1,2,3,0:T(8,128)} async-done(((f32[8,64,2,2,512]{4,1,2,3,0:T(8,128)}), f32[8,64,2,2,512]{4,1,2,3,0:T(8,128)}, u32[]{:S(2)}, u32[]{:S(2)}) %all-to-all-start.1) | async-done | bytes 4194336 | tf_op jit(solution)/shard_map/all_to_all | solution.py:100
  348.8 6.0 %reshape.232 = f32[64,2,2,8,2,256]{5,4,0,1,2,3:T(2,128)} reshape(f32[64,2,2,8,512]{4,0,1,2,3:T(8,128)} %bitcast.14) | data formatting | bytes 8388608 | tf_op jit(solution)/shard_map/reshape | solution.py:103
  354.8 7.8 %fusion.54 = (f32[64,2,2,8,1,256]{5,4,0,1,2,3:T(1,128)S(1)}, f32[64,2,2,8,1,256]{5,4,0,1,2,3:T(1,128)S(1)}) fusion(f32[64,2,2,8,2,256]{5,4,0,1,2,3:T(2,128)} %reshape.232), kind=kLoop, calls=%fused_computation.103 | loop fusion | bytes 8388608 | tf_op jit(solution)/shard_map/slice | solution.py:104
  362.6 2.3 add_bitcast_fusion
  365.4 92.2 %fusion = f32[64,64,1025]{2,1,0:T(8,128)} fusion(f32[64,64,256]{2,1,0:T(8,128)S(1)} %bitcast.150, f32[256,64,1025]{0,1,2:T(8,128)} %param.19), kind=kOutput, calls=%fused_computation | convolution fusion | flops 6448742400 | bytes 88162304 | tf_op jit(solution)/shard_map/dot_general | solution.py:108
  457.6 9.5 %fusion.3 = f32[64,2,8,1025]{3,2,1,0:T(8,128)} fusion(f32[64,2,2,2,8,1025]{5,4,3,2,1,0:T(8,128)} %bitcast.149, pred[64,1025]{1,0:T(8,128)(4,1)S(1)} %get-tuple-element.40, pred[64,1025]{1,0:T(8,128)(4,1)S(1)} %get-tuple-element.39), kind=kLoop, calls=%fused_computation.4 | loop fusion | flops 3148800 | bytes 21123200 | tf_op jit(solution)/shard_map/jit(_where)/select_n | solution.py:120
  467.1 47.2 %reduce-scatter.2.cloned.1.call-done = f32[16,2,8,1025]{3,2,1,0:T(8,128)} async-done(((f32[64,2,8,1025]{3,2,1,0:T(8,128)}), f32[16,2,8,1025]{3,2,1,0:T(8,128)}) %reduce-scatter.2.cloned.1.call-update) | async-done | bytes 1049616 | tf_op jit(solution)/shard_map/reduce_scatter | solution.py:125
  (55 shorter events, 3.9 us)
Async XLA Ops:
  6.5 7.4 %copy-start.3 = (s32[512]{0:T(512)S(1)}, s32[512]{0:T(512)}, u32[]{:S(2)}) copy-start(s32[512]{0:T(512)} %param.20) | copy-start | bytes 6148
  6.5 190.6 %copy-start.4 = (f32[512]{0:T(512)S(1)}, f32[512]{0:T(512)}, u32[]{:S(2)}) copy-start(f32[512]{0:T(512)} %constant.87.clone) | copy-start | bytes 6148
  6.5 190.6 %copy-start.5 = (f32[512]{0:T(512)S(1)}, f32[512]{0:T(512)}, u32[]{:S(2)}) copy-start(f32[512]{0:T(512)} %constant.86.clone) | copy-start | bytes 6148
  6.5 190.6 %all-to-all-start = ((f32[8,512,512]{2,1,0:T(8,128)}), f32[8,512,512]{2,1,0:T(8,128)}, u32[]{:S(2)}, u32[]{:S(2)}) async-start(f32[8,512,512]{2,1,0:T(8,128)} %bitcast.151), calls=%async_computation | async-start | bytes 16777216 | tf_op jit(solution)/shard_map/all_to_all | solution.py:66
  14.1 187.5 %copy-start.8 = (f32[512]{0:T(512)S(1)}, f32[512]{0:T(512)}, u32[]{:S(2)}) copy-start(f32[512]{0:T(512)} %constant.83.clone) | copy-start | bytes 6148
  14.2 187.5 %copy-start.9 = (f32[512]{0:T(512)S(1)}, f32[512]{0:T(512)}, u32[]{:S(2)}) copy-start(f32[512]{0:T(512)} %constant.82.clone) | copy-start | bytes 6148
  14.2 187.5 %copy-start.14 = (f32[512]{0:T(512)S(1)}, f32[512]{0:T(512)}, u32[]{:S(2)}) copy-start(f32[512]{0:T(512)} %constant.80.clone) | copy-start | bytes 6148
  207.4 0.7 copy-start.12
  207.4 0.7 copy-start.13
  208.1 0.7 copy-start.6
  208.1 0.7 copy-start.7
  208.8 4.5 copy-start.10
  208.8 4.5 copy-start.11
  213.3 1.2 copy-start
  213.3 1.2 copy-start.15
  213.3 1.2 copy-start.16
  213.4 1.2 copy-start.17
  215.6 1.2 copy-start.2
  241.9 4.1 copy-start.1
  251.7 97.1 %all-to-all-start.1 = ((f32[8,64,2,2,512]{4,1,2,3,0:T(8,128)}), f32[8,64,2,2,512]{4,1,2,3,0:T(8,128)}, u32[]{:S(2)}, u32[]{:S(2)}) async-start(f32[8,64,2,2,512]{4,1,2,3,0:T(8,128)} %copy.28), calls=%async_computation.1 | async-start | bytes 8388608 | tf_op jit(solution)/shard_map/all_to_all | solution.py:100
  256.3 258.0 %reduce-scatter.2.cloned.1.call-start = ((), (), s32[]{:S(2)}) async-start(), calls=%async_computation.3 | async-start | bytes 5898240 | tf_op jit(solution)/shard_map/reduce_scatter | solution.py:125
Sparse Core Ops, SparseCore 0:
  467.2 47.0 reduce-scatter.1
